TPU v7x, 32 devices: a whole 2x2x4 slice. The times are simulated.
32 devices in a mesh: rows: 8 (over y, x, core), feat: 4 (over z).
Axes of the slice: x: 2, y: 2, z: 4, core: 2. Of those that a mesh axis runs over, the one named last changes fastest.
Arguments:
- features: bfloat16 [8192, 2048], P('rows', 'feat'), may hold values from -6 to 6
- grad_out: bfloat16 [8192, 2048], P('rows', 'feat'), may hold values from -6 to 6
- eigvecs: float32 [2048, 2048], P('feat', 'rows'), may hold values from -1 to 1, as said below
- eigvals: float32 [2048], replicated, may hold values from 0.1 to 1, as said below
- whiten: bfloat16 [2048, 2048], P(None, 'feat'), may hold values from -0.125 to 0.125
Outputs:
- grad_in: bfloat16 [8192, 2048], P('rows', 'feat')
Inputs may be any that keep to these rules, and one draw needn't show every extreme that they name: `eigvecs`: the columns are orthonormal. `eigvals`: any two entries differ by at least 0.45 / 2048.
All inputs are finite; a program needn't handle non-finite values.
Results may differ from a plain program's by a relative error of at most 0.0074.
Values may be sent and summed in bfloat16 or wider, within the bound.
A program may use at most 128 MiB of HBM per device.

v0:
```python
import jax
import jax.numpy as jnp
from jax import lax
from jax.sharding import PartitionSpec as P


def divided(lam_row, lam_col, first_col):
    on_diag = (
        jnp.arange(lam_row.shape[0], dtype=jnp.int32)[:, None]
        == (first_col + jnp.arange(lam_col.shape[0], dtype=jnp.int32))[None, :]
    )
    root_row = lam_row ** (-0.5)
    root_col = lam_col ** (-0.5)
    gaps_lam = lam_row[:, None] - lam_col[None, :]
    safe_gap = jnp.where(on_diag, jnp.ones_like(gaps_lam), gaps_lam)
    off_diag = (root_row[:, None] - root_col[None, :]) / safe_gap
    diag_vals = -0.5 * lam_row[:, None] ** (-1.5) + jnp.zeros_like(gaps_lam)
    return jnp.where(on_diag, diag_vals, off_diag)


def local(features, grad_out, eigvecs, eigvals, whiten):
    highest = lax.Precision.HIGHEST
    tok_rows, own_cols = features.shape
    row_count = tok_rows * lax.axis_size("rows")
    contract_rows = (((0,), (0,)), ((), ()))
    contract_last = (((1,), (1,)), ((), ()))
    piece_x = lax.all_gather(features, "feat", axis=1, tiled=True)
    piece_g = lax.all_gather(grad_out, "feat", axis=1, tiled=True)
    left_part = lax.dot_general(
        features, piece_g, contract_rows, preferred_element_type=jnp.float32
    )
    right_part = lax.dot_general(
        grad_out, piece_x, contract_rows, preferred_element_type=jnp.float32
    )
    cross_one = left_part
    cross_two = right_part
    sum_x = jnp.sum(piece_x, axis=0, dtype=jnp.float32)
    sum_g = jnp.sum(piece_g, axis=0, dtype=jnp.float32)
    cross_one, cross_two, sum_x, sum_g = (cross_one, cross_two, sum_x, sum_g)
    cross_one, cross_two, sum_x, sum_g = lax.psum((cross_one, cross_two, sum_x, sum_g), "rows")
    both_cross = cross_one + cross_two
    col_mean = sum_x / row_count
    grad_mean = sum_g / row_count
    offset = lax.axis_index("feat") * own_cols
    mean_part = lax.dynamic_slice_in_dim(col_mean, offset, own_cols)
    grad_part = lax.dynamic_slice_in_dim(grad_mean, offset, own_cols)
    sym_gram = 0.5 * (
        both_cross
        - row_count
        * (mean_part[:, None] * grad_mean[None, :] + grad_part[:, None] * col_mean[None, :])
    )
    basis_cols = lax.all_gather(eigvecs, "feat", axis=0, tiled=True)
    basis_block = lax.all_gather(eigvecs, "rows", axis=1, tiled=True)
    narrow = basis_cols.shape[1]
    inner_prod = jnp.dot(sym_gram, basis_cols, precision=highest)
    partial_value = lax.dot_general(basis_block, inner_prod, contract_rows, precision=highest)
    rotated = lax.psum(partial_value, "feat")
    first_col = lax.axis_index("rows") * narrow
    lam_col = lax.dynamic_slice_in_dim(eigvals, first_col, narrow)
    scaled = divided(eigvals, lam_col, first_col) * rotated
    back_rot = jnp.dot(basis_block, scaled, precision=highest)
    sens_own = lax.psum_scatter(
        lax.dot_general(back_rot, basis_cols, contract_last, precision=highest),
        "rows",
        scatter_dimension=0,
        tiled=True,
    )
    scaled_own = (2.0 / row_count * sens_own).astype(jnp.bfloat16)
    sens_scaled = lax.all_gather(scaled_own, "rows", axis=0, tiled=True)
    piece_x = lax.all_gather(features, "feat", axis=1, tiled=True)
    piece_g = lax.all_gather(grad_out, "feat", axis=1, tiled=True)
    shifted = (piece_g.astype(jnp.float32) - grad_mean).astype(jnp.bfloat16)
    centered = (piece_x.astype(jnp.float32) - col_mean).astype(jnp.bfloat16)
    running = jnp.dot(shifted, whiten, preferred_element_type=jnp.float32)
    grad_in = running + lax.dot_general(
        centered, sens_scaled, contract_last, preferred_element_type=jnp.float32
    )
    return grad_in.astype(jnp.bfloat16)


def solution(mesh):
    in_specs = (P("rows", "feat"), P("rows", "feat"), P("feat", "rows"), P(), P(None, "feat"))
    out_specs = P("rows", "feat")
    return jax.shard_map(local, mesh=mesh, in_specs=in_specs, out_specs=out_specs, check_vma=False)
```

profile of v0, /device:TPU:0, one launch (start us, length us, event | category | flops | bytes accessed | tf_op | source)
XLA Modules:
  0.0 552.3 jit_solution(13871746332786428748)
XLA Ops:
  6.5 0.0 copy-start
  6.5 0.0 all-gather.6.cloned.1.call-start
  6.5 0.7 all-gather.6.cloned.1.call-update
  7.3 0.0 all-gather.8.cloned.1.call-start
  7.3 0.7 all-gather.8.cloned.1.call-update
  8.0 0.0 all-gather.10.cloned.1.call-start
  8.1 0.7 all-gather.10.cloned.1.call-update
  8.7 0.0 copy-start.3
  8.8 0.0 all-reduce.6.cloned.1.call-start
  8.8 83.6 %all-gather.6.cloned.1.call-done = bf16[1024,2048]{1,0:T(8,128)(2,1)} async-done(((bf16[1024,512]{1,0:T(8,128)(2,1)}), bf16[1024,2048]{1,0:T(8,128)(2,1)}) %all-gather.6.cloned.1.call-update) | async-done | bytes 4194320 | tf_op jit(solution)/shard_map/all_gather | solution.py:71
  92.4 6.8 %fusion.40 = f32[512,2048]{1,0:T(8,128)} fusion(bf16[1024,512]{1,0:T(8,128)(2,1)} %param.5, bf16[1024,2048]{1,0:T(8,128)(2,1)} %all-gather.6.cloned.1.call-done), kind=kOutput, calls=%fused_computation.51 | convolution fusion | flops 2147483648 | bytes 9437184 | tf_op jit(solution)/shard_map/dot_general | solution.py:29
  99.2 74.0 %all-gather.8.cloned.1.call-done = bf16[1024,2048]{1,0:T(8,128)(2,1)} async-done(((bf16[1024,512]{1,0:T(8,128)(2,1)}), bf16[1024,2048]{1,0:T(8,128)(2,1)}) %all-gather.8.cloned.1.call-update) | async-done | bytes 4194320 | tf_op jit(solution)/shard_map/all_gather | solution.py:70
  173.2 0.0 copy-done.3
  173.2 7.8 %convolution_add_fusion = f32[512,2048]{1,0:T(8,128)} fusion(f32[512,2048]{1,0:T(8,128)} %fusion.40, bf16[1024,512]{1,0:T(8,128)(2,1)S(1)} %copy-done.3, bf16[1024,2048]{1,0:T(8,128)(2,1)} %all-gather.8.cloned.1.call-done), kind=kOutput, calls=%fused_computation.17 | convolution fusion | flops 2148532224 | bytes 13631488 | tf_op jit(solution)/shard_map/dot_general | solution.py:32
  181.0 0.0 all-reduce.6.cloned.1.call-update
  181.1 0.0 all-gather.12.cloned.1.call-start
  181.1 0.5 all-gather.12.cloned.1.call-update
  181.7 0.0 all-reduce.4.cloned.1.call-start
  181.7 0.0 copy-start.1
  181.7 3.0 convert_reduce_fusion
  184.7 0.5 copy-done.1
  185.2 0.6 convert_reduce_fusion.1
  185.8 25.6 %all-reduce = (f32[2048]{0:T(1024)S(1)}, f32[2048]{0:T(1024)S(1)}) all-reduce(f32[2048]{0:T(1024)S(1)} %convert_reduce_fusion, f32[2048]{0:T(1024)S(1)} %convert_reduce_fusion.1), channel_id=1, replica_groups=mesh['rows'=8,'feat'=4] {'rows'}, use_global_device_ids=true, to_apply=%region_3.0 | all-reduce | flops 4096 | bytes 32768 | tf_op jit(solution)/shard_map/psum | solution.py:40
  211.4 0.1 dynamic_slice.10
  211.5 0.1 dynamic_slice.11
  211.6 7.4 %all-gather.10.cloned.1.call-done = f32[2048,256]{1,0:T(8,128)} async-done(((f32[512,256]{1,0:T(8,128)}), f32[2048,256]{1,0:T(8,128)}) %all-gather.10.cloned.1.call-update) | async-done | bytes 2097168 | tf_op jit(solution)/shard_map/all_gather | solution.py:52
  219.0 82.8 %all-reduce.6.cloned.1.call-done = f32[512,2048]{1,0:T(8,128)} async-done(((f32[512,2048]{1,0:T(8,128)}), f32[512,2048]{1,0:T(8,128)}) %all-reduce.6.cloned.1.call-update) | async-done | bytes 4194320 | tf_op jit(solution)/shard_map/psum | solution.py:40
  301.7 6.9 %fusion.6 = f32[512,256]{1,0:T(8,128)S(1)} fusion(f32[2048,256]{1,0:T(8,128)} %all-gather.10.cloned.1.call-done, f32[512,2048]{1,0:T(8,128)} %all-reduce.6.cloned.1.call-done, f32[2048]{0:T(1024)S(1)} %get-tuple-element.11, f32[512]{0:T(512)S(1)} %dynamic_slice.11, f32[2048]{0:T(1024)S(1)} %get-tuple-element.12, f32[512]{0:T(512)S(1)} %dynamic_slice.10), kind=kOutput, calls=%fused_computation.8 | convolution fusion | flops 3227516928 | bytes 6836224 | tf_op jit(solution)/shard_map/dot_general | solution.py:55
  308.6 0.0 copy-start.5
  308.6 32.3 %all-gather.12.cloned.1.call-done = f32[512,2048]{1,0:T(8,128)} async-done(((f32[512,256]{1,0:T(8,128)}), f32[512,2048]{1,0:T(8,128)}) %all-gather.12.cloned.1.call-update) | async-done | bytes 4194320 | tf_op jit(solution)/shard_map/all_gather | solution.py:53
  340.9 10.2 %convolution_bitcast_fusion = f32[2048,256]{1,0:T(8,128)} fusion(f32[512,256]{1,0:T(8,128)S(1)} %fusion.6, f32[512,2048]{1,0:T(8,128)} %all-gather.12.cloned.1.call-done), kind=kOutput, calls=%fused_computation.18 | convolution fusion | flops 3221225472 | bytes 6815744 | tf_op jit(solution)/shard_map/dot_general | solution.py:56
  351.1 0.0 all-reduce.4.cloned.1.call-update
  351.1 0.3 reduce-scatter.2.cloned.1.call-start
  351.4 0.0 copy-done.5
  351.4 0.1 broadcast_power_fusion.1
  351.5 85.9 %all-reduce.4.cloned.1.call-done = f32[2048,256]{1,0:T(8,128)} async-done(((f32[2048,256]{1,0:T(8,128)}), f32[2048,256]{1,0:T(8,128)}) %all-reduce.4.cloned.1.call-update) | async-done | bytes 2097168 | tf_op jit(solution)/shard_map/psum | solution.py:57
  437.4 0.0 copy-start.4
  437.4 10.8 %fusion.15 = f32[256,512]{1,0:T(8,128)S(1)} fusion(f32[512,2048]{1,0:T(8,128)} %all-gather.12.cloned.1.call-done, f32[2048,256]{1,0:T(8,128)} %all-reduce.4.cloned.1.call-done, f32[256]{0:T(256)S(1)} %get-tuple-element.8, f32[2048]{0:T(1024)S(1)} %copy-done.5, f32[256]{0:T(256)S(1)} %get-tuple-element.7, f32[2048]{0:T(1024)S(1)} %get-tuple-element.10, ...), kind=kOutput, calls=%fused_computation.20 | convolution fusion | flops 3224895488 | bytes 6843392 | tf_op jit(solution)/shard_map/dot_general | solution.py:61
  448.2 0.0 copy-done.4
  448.2 8.4 %fusion.41 = f32[512,2048]{1,0:T(8,128)} fusion(f32[256,512]{1,0:T(8,128)S(1)} %fusion.15, f32[2048,256]{1,0:T(8,128)S(1)} %copy-done.4), kind=kOutput, calls=%fused_computation.52 | convolution fusion | flops 3221225472 | bytes 6815744 | tf_op jit(solution)/shard_map/dot_general | solution.py:63
  456.6 0.0 reduce-scatter.2.cloned.1.call-update
  456.7 0.3 all-gather.14.cloned.1.call-start
  457.0 50.0 %reduce-scatter.2.cloned.1.call-done = f32[64,2048]{1,0:T(8,128)} async-done(((f32[512,2048]{1,0:T(8,128)}), f32[64,2048]{1,0:T(8,128)}) %reduce-scatter.2.cloned.1.call-update) | async-done | bytes 524304 | tf_op jit(solution)/shard_map/reduce_scatter | solution.py:62
  507.0 1.8 multiply_convert_fusion
  508.8 0.0 all-gather.14.cloned.1.call-update
  508.8 27.9 %all-gather.14.cloned.1.call-done = bf16[512,2048]{1,0:T(8,128)(2,1)} async-done(((bf16[64,2048]{1,0:T(8,128)(2,1)}), bf16[512,2048]{1,0:T(8,128)(2,1)}) %all-gather.14.cloned.1.call-update) | async-done | bytes 2097168 | tf_op jit(solution)/shard_map/all_gather | solution.py:69
  536.7 0.0 copy-start.2
  536.7 5.4 fusion.2
  542.1 0.0 copy-done
  542.1 0.0 copy-done.2
  542.1 3.3 add_convert_fusion
  (3 shorter events, 0.0 us)
Async XLA Ops:
  6.5 535.6 %copy-start = (bf16[2048,512]{1,0:T(8,128)(2,1)S(1)}, bf16[2048,512]{1,0:T(8,128)(2,1)}, u32[]{:S(2)}) copy-start(bf16[2048,512]{1,0:T(8,128)(2,1)} %param.9) | copy-start | bytes 6291460
  6.5 85.9 %all-gather.6.cloned.1.call-start = ((), (), s32[]{:S(2)}) async-start(), calls=%async_computation.1 | async-start | bytes 5242880 | tf_op jit(solution)/shard_map/all_gather | solution.py:71
  7.3 166.0 %all-gather.8.cloned.1.call-start = ((), (), s32[]{:S(2)}) async-start(), calls=%async_computation.2 | async-start | bytes 5242880 | tf_op jit(solution)/shard_map/all_gather | solution.py:70
  8.0 211.0 %all-gather.10.cloned.1.call-start = ((), (), s32[]{:S(2)}) async-start(), calls=%async_computation.3 | async-start | bytes 2621440 | tf_op jit(solution)/shard_map/all_gather | solution.py:52
  8.7 164.5 %copy-start.3 = (bf16[1024,512]{1,0:T(8,128)(2,1)S(1)}, bf16[1024,512]{1,0:T(8,128)(2,1)}, u32[]{:S(2)}) copy-start(bf16[1024,512]{1,0:T(8,128)(2,1)} %param.6) | copy-start | bytes 3145732
  8.8 293.0 %all-reduce.6.cloned.1.call-start = ((), (), s32[]{:S(2)}) async-start(), calls=%async_computation.8 | async-start | bytes 8388608 | tf_op jit(solution)/shard_map/psum | solution.py:40
  181.1 159.9 %all-gather.12.cloned.1.call-start = ((), (), s32[]{:S(2)}) async-start(), calls=%async_computation.4 | async-start | bytes 4718592 | tf_op jit(solution)/shard_map/all_gather | solution.py:53
  181.7 255.8 %all-reduce.4.cloned.1.call-start = ((), (), s32[]{:S(2)}) async-start(), calls=%async_computation.5 | async-start | bytes 4194304 | tf_op jit(solution)/shard_map/psum | solution.py:57
  181.7 3.5 copy-start.1
  308.6 42.8 %copy-start.5 = (f32[2048]{0:T(1024)S(1)}, f32[2048]{0:T(1024)}, u32[]{:S(2)}) copy-start(f32[2048]{0:T(1024)} %param.8) | copy-start | bytes 24580
  351.1 155.9 %reduce-scatter.2.cloned.1.call-start = ((), (), s32[]{:S(2)}) async-start(), calls=%async_computation.6 | async-start | bytes 4718592 | tf_op jit(solution)/shard_map/reduce_scatter | solution.py:62
  437.4 10.8 %copy-start.4 = (f32[2048,256]{1,0:T(8,128)S(1)}, f32[2048,256]{1,0:T(8,128)}, u32[]{:S(2)}) copy-start(f32[2048,256]{1,0:T(8,128)} %all-gather.10.cloned.1.call-done) | copy-start | bytes 6291460
  456.7 80.1 %all-gather.14.cloned.1.call-start = ((), (), s32[]{:S(2)}) async-start(), calls=%async_computation.7 | async-start | bytes 2359296 | tf_op jit(solution)/shard_map/all_gather | solution.py:69
  536.7 5.4 copy-start.2
Sparse Core Ops, SparseCore 0:
  8.9 83.4 all-gather.5
  94.0 79.2 all-gather.7
  174.8 44.1 all-gather.9
  222.1 79.5 all-reduce.5
  303.5 37.3 all-gather.11
  351.3 86.1 all-reduce.3
  456.8 50.1 reduce-scatter.1
  508.9 27.7 all-gather.13
where the time goes:
time: 552 us
  waiting for transfers between devices  447 us (81%)
  matrix products  59.6 us (11%)
  blocking collectives  25.6 us (5%)
  between operations  13.6 us (2%)
    psum x1, waiting for transfers between devices, local(): rotated = lax.psum(partial_value, 'feat')  85.9 us
    all_gather x1, waiting for transfers between devices, local(): piece_g = lax.all_gather(grad_out, 'feat', axis=1, tiled=True)  83.6 us
    psum x1, waiting for transfers between devices, local(): lax.psum((cross_one, cross_two, sum_x, sum_g), 'rows')  82.8 us
    all_gather x1, waiting for transfers between devices, local(): piece_x = lax.all_gather(features, 'feat', axis=1, tiled=True)  74 us
    reduce_scatter x1, waiting for transfers between devices, local(): lax.psum_scatter(lax.dot_general(back_rot, basis_cols, contract_last, pre...  50 us
    all_gather x1, waiting for transfers between devices, local(): basis_block = lax.all_gather(eigvecs, 'rows', axis=1, tiled=True)  32.3 us
    all_gather x1, waiting for transfers between devices, local(): sens_scaled = lax.all_gather(scaled_own, 'rows', axis=0, tiled=True)  27.9 us
    psum x1, blocking collectives, local(): lax.psum((cross_one, cross_two, sum_x, sum_g), 'rows')  25.6 us
  transfers between devices with their start and end apart: 8, of which 8 were waited for; matrix products, arithmetic and copies ran while one was open for 5% of the time, Pallas kernels for 0%

commit v1 on v0

--- a/solution.py
+++ b/solution.py
@@ -2,6 +2,7 @@
 import jax.numpy as jnp
 from jax import lax
 from jax.sharding import PartitionSpec as P
+from jax.lax import all_gather
 
 
 def divided(lam_row, lam_col, first_col):
@@ -67,8 +68,11 @@
     )
     scaled_own = (2.0 / row_count * sens_own).astype(jnp.bfloat16)
     sens_scaled = lax.all_gather(scaled_own, "rows", axis=0, tiled=True)
-    piece_x = lax.all_gather(features, "feat", axis=1, tiled=True)
-    piece_g = lax.all_gather(grad_out, "feat", axis=1, tiled=True)
+    piece_x, piece_g = jnp.split(
+        all_gather(jnp.concatenate([features, grad_out], axis=0), "feat", axis=1, tiled=True),
+        [features.shape[0]],
+        axis=0,
+    )
     shifted = (piece_g.astype(jnp.float32) - grad_mean).astype(jnp.bfloat16)
     centered = (piece_x.astype(jnp.float32) - col_mean).astype(jnp.bfloat16)
     running = jnp.dot(shifted, whiten, preferred_element_type=jnp.float32)

time: 552 us -> 700 us (1.27)
  waiting for transfers between devices: 447 us -> 587 us
    all_gather x0 -> x1, waiting for transfers between devices: none -> 149 us  [local(): all_gather(jnp.concatenate([features, grad_out], axis=0), 'feat', axis=1,...]
  transfers between devices with their start and end apart: 8 -> 9, of which waited for: 8 -> 9; matrix products, arithmetic and copies ran while one was open for 5% -> 5% of each run, Pallas kernels for 0% -> 0%
where the time goes in v1:
time: 700 us; the launch traced here: 699 us
  waiting for transfers between devices  587 us (84%)
  matrix products  63.4 us (9%)
  blocking collectives  25.6 us (4%)
  between operations  13.3 us (2%)
  other arithmetic  8.14 us (1%)
    all_gather x1, waiting for transfers between devices, local(): all_gather(jnp.concatenate([features, grad_out], axis=0), 'feat', axis=1,...  149 us
    psum x1, waiting for transfers between devices, local(): rotated = lax.psum(partial_value, 'feat')  85.9 us
    all_gather x1, waiting for transfers between devices, local(): piece_g = lax.all_gather(grad_out, 'feat', axis=1, tiled=True)  83.6 us
    psum x1, waiting for transfers between devices, local(): lax.psum((cross_one, cross_two, sum_x, sum_g), 'rows')  82.8 us
    all_gather x1, waiting for transfers between devices, local(): piece_x = lax.all_gather(features, 'feat', axis=1, tiled=True)  74 us
    reduce_scatter x1, waiting for transfers between devices, local(): lax.psum_scatter(lax.dot_general(back_rot, basis_cols, contract_last, pre...  47.2 us
    all_gather x1, waiting for transfers between devices, local(): basis_block = lax.all_gather(eigvecs, 'rows', axis=1, tiled=True)  32.3 us
    psum x1, blocking collectives, local(): lax.psum((cross_one, cross_two, sum_x, sum_g), 'rows')  25.6 us
  transfers between devices with their start and end apart: 9, of which 9 were waited for; matrix products, arithmetic and copies ran while one was open for 5% of the time, Pallas kernels for 0%

profile of v1, /device:TPU:0, one launch (start us, length us, event | category | flops | bytes accessed | tf_op | source)
XLA Modules:
  0.0 699.4 jit_solution(9084135493678189630)
XLA Ops:
  6.5 0.0 copy-start
  6.5 0.0 all-gather.9.cloned.1.call-start
  6.5 0.7 all-gather.9.cloned.1.call-update
  7.3 0.0 all-gather.11.cloned.1.call-start
  7.3 0.7 all-gather.11.cloned.1.call-update
  8.0 0.0 all-gather.13.cloned.1.call-start
  8.1 0.7 all-gather.13.cloned.1.call-update
  8.7 0.0 copy-start.3
  8.8 0.0 all-reduce.6.cloned.1.call-start
  8.8 83.6 %all-gather.9.cloned.1.call-done = bf16[1024,2048]{1,0:T(8,128)(2,1)} async-done(((bf16[1024,512]{1,0:T(8,128)(2,1)}), bf16[1024,2048]{1,0:T(8,128)(2,1)}) %all-gather.9.cloned.1.call-update) | async-done | bytes 4194320 | tf_op jit(solution)/shard_map/all_gather | solution.py:29
  92.4 6.8 fusion.36
  99.2 74.0 %all-gather.11.cloned.1.call-done = bf16[1024,2048]{1,0:T(8,128)(2,1)} async-done(((bf16[1024,512]{1,0:T(8,128)(2,1)}), bf16[1024,2048]{1,0:T(8,128)(2,1)}) %all-gather.11.cloned.1.call-update) | async-done | bytes 4194320 | tf_op jit(solution)/shard_map/all_gather | solution.py:28
  173.2 0.0 copy-done.3
  173.2 7.8 %convolution_add_fusion = f32[512,2048]{1,0:T(8,128)} fusion(f32[512,2048]{1,0:T(8,128)} %fusion.36, bf16[1024,512]{1,0:T(8,128)(2,1)S(1)} %copy-done.3, bf16[1024,2048]{1,0:T(8,128)(2,1)} %all-gather.11.cloned.1.call-done), kind=kOutput, calls=%fused_computation.17 | convolution fusion | flops 2148532224 | bytes 13631488 | tf_op jit(solution)/shard_map/dot_general | solution.py:33
  181.0 0.0 all-reduce.6.cloned.1.call-update
  181.0 0.0 all-gather.15.cloned.1.call-start
  181.1 0.5 all-gather.15.cloned.1.call-update
  181.6 0.0 all-reduce.4.cloned.1.call-start
  181.7 0.0 copy-start.1
  181.7 3.0 convert_reduce_fusion
  184.7 0.5 copy-done.1
  185.2 0.6 convert_reduce_fusion.1
  185.8 25.6 %all-reduce = (f32[2048]{0:T(1024)S(1)}, f32[2048]{0:T(1024)S(1)}) all-reduce(f32[2048]{0:T(1024)S(1)} %convert_reduce_fusion.1, f32[2048]{0:T(1024)S(1)} %convert_reduce_fusion), channel_id=1, replica_groups=mesh['rows'=8,'feat'=4] {'rows'}, use_global_device_ids=true, to_apply=%region_1.0 | all-reduce | flops 4096 | bytes 32768 | tf_op jit(solution)/shard_map/psum | solution.py:41
  211.4 0.1 dynamic_slice.10
  211.5 0.1 dynamic_slice.11
  211.6 7.4 %all-gather.13.cloned.1.call-done = f32[2048,256]{1,0:T(8,128)} async-done(((f32[512,256]{1,0:T(8,128)}), f32[2048,256]{1,0:T(8,128)}) %all-gather.13.cloned.1.call-update) | async-done | bytes 2097168 | tf_op jit(solution)/shard_map/all_gather | solution.py:53
  219.0 82.8 %all-reduce.6.cloned.1.call-done = f32[512,2048]{1,0:T(8,128)} async-done(((f32[512,2048]{1,0:T(8,128)}), f32[512,2048]{1,0:T(8,128)}) %all-reduce.6.cloned.1.call-update) | async-done | bytes 4194320 | tf_op jit(solution)/shard_map/psum | solution.py:41
  301.8 6.9 fusion.4
  308.6 0.0 copy-start.5
  308.6 32.3 %all-gather.15.cloned.1.call-done = f32[512,2048]{1,0:T(8,128)} async-done(((f32[512,256]{1,0:T(8,128)}), f32[512,2048]{1,0:T(8,128)}) %all-gather.15.cloned.1.call-update) | async-done | bytes 4194320 | tf_op jit(solution)/shard_map/all_gather | solution.py:54
  340.9 10.2 %convolution_bitcast_fusion = f32[2048,256]{1,0:T(8,128)} fusion(f32[512,256]{1,0:T(8,128)S(1)} %fusion.4, f32[512,2048]{1,0:T(8,128)} %all-gather.15.cloned.1.call-done), kind=kOutput, calls=%fused_computation.18 | convolution fusion | flops 3221225472 | bytes 6815744 | tf_op jit(solution)/shard_map/dot_general | solution.py:57
  351.1 0.0 all-reduce.4.cloned.1.call-update
  351.1 0.3 reduce-scatter.2.cloned.1.call-start
  351.4 0.0 copy-done.5
  351.4 0.1 broadcast_power_fusion.1
  351.5 85.9 %all-reduce.4.cloned.1.call-done = f32[2048,256]{1,0:T(8,128)} async-done(((f32[2048,256]{1,0:T(8,128)}), f32[2048,256]{1,0:T(8,128)}) %all-reduce.4.cloned.1.call-update) | async-done | bytes 2097168 | tf_op jit(solution)/shard_map/psum | solution.py:58
  437.4 0.0 copy-start.4
  437.4 10.8 %fusion.13 = f32[256,512]{1,0:T(8,128)S(1)} fusion(f32[512,2048]{1,0:T(8,128)} %all-gather.15.cloned.1.call-done, f32[2048,256]{1,0:T(8,128)} %all-reduce.4.cloned.1.call-done, f32[256]{0:T(256)S(1)} %get-tuple-element.8, f32[2048]{0:T(1024)S(1)} %copy-done.5, f32[256]{0:T(256)S(1)} %get-tuple-element.7, f32[2048]{0:T(1024)S(1)} %get-tuple-element.10, ...), kind=kOutput, calls=%fused_computation.21 | convolution fusion | flops 3224895488 | bytes 6843392 | tf_op jit(solution)/shard_map/dot_general | solution.py:62
  448.2 0.0 copy-done.4
  448.2 0.0 copy-start.2
  448.2 8.3 %fusion.37 = f32[512,2048]{1,0:T(8,128)} fusion(f32[256,512]{1,0:T(8,128)S(1)} %fusion.13, f32[2048,256]{1,0:T(8,128)S(1)} %copy-done.4), kind=kOutput, calls=%fused_computation.53 | convolution fusion | flops 3221225472 | bytes 6815744 | tf_op jit(solution)/shard_map/dot_general | solution.py:64
  456.6 0.0 reduce-scatter.2.cloned.1.call-update
  456.6 0.0 all-gather.7.cloned.1.call-start
  456.7 0.0 copy-done.2
  456.7 2.7 pad_maximum_fusion
  459.4 0.0 all-gather.7.cloned.1.call-update
  459.4 0.3 all-gather.17.cloned.1.call-start
  459.7 47.2 %reduce-scatter.2.cloned.1.call-done = f32[64,2048]{1,0:T(8,128)} async-done(((f32[512,2048]{1,0:T(8,128)}), f32[64,2048]{1,0:T(8,128)}) %reduce-scatter.2.cloned.1.call-update) | async-done | bytes 524304 | tf_op jit(solution)/shard_map/reduce_scatter | solution.py:63
  507.0 1.8 multiply_convert_fusion
  508.7 0.0 all-gather.17.cloned.1.call-update
  508.8 149.4 %all-gather.7.cloned.1.call-done = bf16[2048,2048]{1,0:T(8,128)(2,1)} async-done(((bf16[2048,512]{1,0:T(8,128)(2,1)}), bf16[2048,2048]{1,0:T(8,128)(2,1)}) %all-gather.7.cloned.1.call-update) | async-done | bytes 8388624 | tf_op jit(solution)/shard_map/all_gather | solution.py:72
  658.2 0.0 copy-done
  658.2 5.9 fusion
  664.0 22.0 %all-gather.17.cloned.1.call-done = bf16[512,2048]{1,0:T(8,128)(2,1)} async-done(((bf16[64,2048]{1,0:T(8,128)(2,1)}), bf16[512,2048]{1,0:T(8,128)(2,1)}) %all-gather.17.cloned.1.call-update) | async-done | bytes 2097168 | tf_op jit(solution)/shard_map/all_gather | solution.py:70
  686.1 6.8 add_convert_fusion
  (3 shorter events, 0.0 us)
Async XLA Ops:
  6.5 651.6 %copy-start = (bf16[2048,512]{1,0:T(8,128)(2,1)S(1)}, bf16[2048,512]{1,0:T(8,128)(2,1)}, u32[]{:S(2)}) copy-start(bf16[2048,512]{1,0:T(8,128)(2,1)} %param.9) | copy-start | bytes 6291460
  6.5 85.9 %all-gather.9.cloned.1.call-start = ((), (), s32[]{:S(2)}) async-start(), calls=%async_computation.2 | async-start | bytes 5242880 | tf_op jit(solution)/shard_map/all_gather | solution.py:29
  7.3 166.0 %all-gather.11.cloned.1.call-start = ((), (), s32[]{:S(2)}) async-start(), calls=%async_computation.3 | async-start | bytes 5242880 | tf_op jit(solution)/shard_map/all_gather | solution.py:28
  8.0 211.0 %all-gather.13.cloned.1.call-start = ((), (), s32[]{:S(2)}) async-start(), calls=%async_computation.4 | async-start | bytes 2621440 | tf_op jit(solution)/shard_map/all_gather | solution.py:53
  8.7 164.5 %copy-start.3 = (bf16[1024,512]{1,0:T(8,128)(2,1)S(1)}, bf16[1024,512]{1,0:T(8,128)(2,1)}, u32[]{:S(2)}) copy-start(bf16[1024,512]{1,0:T(8,128)(2,1)} %param.6) | copy-start | bytes 3145732
  8.8 293.0 %all-reduce.6.cloned.1.call-start = ((), (), s32[]{:S(2)}) async-start(), calls=%async_computation.9 | async-start | bytes 8388608 | tf_op jit(solution)/shard_map/psum | solution.py:41
  181.0 159.9 %all-gather.15.cloned.1.call-start = ((), (), s32[]{:S(2)}) async-start(), calls=%async_computation.5 | async-start | bytes 4718592 | tf_op jit(solution)/shard_map/all_gather | solution.py:54
  181.6 255.8 %all-reduce.4.cloned.1.call-start = ((), (), s32[]{:S(2)}) async-start(), calls=%async_computation.6 | async-start | bytes 4194304 | tf_op jit(solution)/shard_map/psum | solution.py:58
  181.7 3.5 copy-start.1
  308.6 42.8 %copy-start.5 = (f32[2048]{0:T(1024)S(1)}, f32[2048]{0:T(1024)}, u32[]{:S(2)}) copy-start(f32[2048]{0:T(1024)} %param.8) | copy-start | bytes 24580
  351.1 155.8 %reduce-scatter.2.cloned.1.call-start = ((), (), s32[]{:S(2)}) async-start(), calls=%async_computation.7 | async-start | bytes 4718592 | tf_op jit(solution)/shard_map/reduce_scatter | solution.py:63
  437.4 10.8 %copy-start.4 = (f32[2048,256]{1,0:T(8,128)S(1)}, f32[2048,256]{1,0:T(8,128)}, u32[]{:S(2)}) copy-start(f32[2048,256]{1,0:T(8,128)} %all-gather.13.cloned.1.call-done) | copy-start | bytes 6291460
  448.2 8.4 %copy-start.2 = (bf16[1024,512]{1,0:T(8,128)(2,1)S(1)}, bf16[1024,512]{1,0:T(8,128)(2,1)}, u32[]{:S(2)}) copy-start(bf16[1024,512]{1,0:T(8,128)(2,1)} %param.5) | copy-start | bytes 3145732
  456.6 201.6 %all-gather.7.cloned.1.call-start = ((), (), s32[]{:S(2)}) async-start(), calls=%async_computation.1 | async-start | bytes 10485760 | tf_op jit(solution)/shard_map/all_gather | solution.py:72
  459.4 226.7 %all-gather.17.cloned.1.call-start = ((), (), s32[]{:S(2)}) async-start(), calls=%async_computation.8 | async-start | bytes 2359296 | tf_op jit(solution)/shard_map/all_gather | solution.py:70
Sparse Core Ops, SparseCore 0:
  8.9 83.4 all-gather.8
  94.0 79.2 all-gather.10
  174.8 44.1 all-gather.12
  222.1 79.5 all-reduce.5
  303.5 37.3 all-gather.14
  351.3 86.1 all-reduce.3
  456.7 50.1 reduce-scatter.1
  508.5 149.6 all-gather.6
  660.1 25.9 all-gather.16
